TPU v7x, 512 devices: a 4x2x32 block of a 4x16x32 slice. The times are simulated.
512 devices in a mesh: parts: 2 (over y), row: 32 (over z), col: 4 (over x), sub: 2 (over core).
Axes of the slice: x: 4, y: 2, z: 32, core: 2. Of those that a mesh axis runs over, the one named last changes fastest.
The devices are a block of a 4x16x32 slice.
Arguments:
- pair: float32 [768, 384, 128], P(('parts', 'row'), ('col', 'sub')), parts along dimension 0, may hold values from -250 to 250, as said below
- residue_mask: int32 [768], P('parts'), parts along dimension 0, may hold values from 0 to 1, as said below
- tri_norm_gain: float32 [128], replicated, may hold values from 0.25 to 1.75
- tri_in_weight: bfloat16 [128, 4, 128], replicated, may hold values from -0.5 to 0.5
- tri_gate_weight: bfloat16 [128, 128], replicated, may hold values from -0.5 to 0.5
- tri_out_norm_gain: float32 [128], replicated, may hold values from 0.25 to 1.75
- tri_out_weight: bfloat16 [128, 128], replicated, may hold values from -0.5 to 0.5
- att_norm_gain: float32 [128], replicated, may hold values from 0.25 to 1.75
- att_proj_weight: bfloat16 [128, 4, 128], replicated, may hold values from -0.5 to 0.5
- att_bias_weight: bfloat16 [128, 4], replicated, may hold values from -15 to 15
- att_out_weight: bfloat16 [128, 128], replicated, may hold values from -0.5 to 0.5
Outputs:
- pair_out: float32 [768, 384, 128], P(('parts', 'row'), ('col', 'sub')), parts along dimension 0
There are 2 independent parts, one for each index of `parts`. A program takes and returns all parts, laid end to end along the dimension named above; an argument that names none is the same for every part. Nothing has to cross between parts.
Inputs may be any that keep to these rules, and one draw needn't show every extreme that they name: The pair entries are finite. `residue_mask`: 0 on every residue at or above a length of at least 192 and less than 384; below it 1, except some unresolved residues that are 0; residue 0 is always 1.
All inputs are finite; a program needn't handle non-finite values.
Results may differ from a plain program's by a relative error of at most 0.0032.
Values may be sent and summed in bfloat16 or wider, within the bound.
A program may use at most 64 MiB of HBM per device.

v0:
```python
import math
import jax
import jax.numpy as jnp
from jax import lax
from jax.sharding import PartitionSpec as P

epsilon = 1e-05
mask_penalty = 1000000000.0


def split_up(array, dim, devices):
    lengths = array.shape
    pieces = array.reshape(*lengths[:dim], devices, lengths[dim] // devices, *lengths[dim + 1 :])
    return jnp.moveaxis(pieces, dim, 0)


def sum_at_owner(array, axis, dim):
    devices = lax.axis_size(axis)
    pieces = lax.all_to_all(split_up(array, dim, devices), axis, 0, 0, tiled=True)
    return jnp.sum(pieces, axis=0)


def in_one_piece(arrays, axis, dim, along):
    widths = [a.shape[along] for a in arrays]
    both = jnp.concatenate(arrays, axis=along)
    result = lax.all_gather(both, axis, axis=dim, tiled=True)
    return tuple(jnp.split(result, [sum(widths[:k]) for k in range(1, len(widths))], axis=along))


def from_everyone(array, axis):
    copies = jnp.broadcast_to(array, (lax.axis_size(axis), *array.shape))
    return lax.all_to_all(copies, axis, split_axis=0, concat_axis=0, tiled=True)


def laid_out(pieces, dim):
    lengths = list(pieces.shape[1:])
    lengths[dim] *= pieces.shape[0]
    return jnp.moveaxis(pieces, 0, dim).reshape(lengths)


def gathered_copies(array, axis, dim):
    pieces = from_everyone(array, axis)
    return laid_out(pieces, dim)


def norm_last(values_in, gain):
    center = jnp.mean(values_in, axis=-1, keepdims=True)
    centered = values_in - center
    variance = jnp.mean(centered * centered, axis=-1, keepdims=True)
    return centered * lax.rsqrt(variance + epsilon) * gain


def project(normed, weight):
    flat_rows = normed.reshape(-1, normed.shape[-1])
    product = jnp.dot(flat_rows, weight, preferred_element_type=jnp.float32)
    return product.reshape(normed.shape[:-1] + (weight.shape[1],))


def body(
    pair,
    residue_mask,
    tri_norm_gain,
    tri_in_weight,
    tri_gate_weight,
    tri_out_norm_gain,
    tri_out_weight,
    att_norm_gain,
    att_proj_weight,
    att_bias_weight,
    att_out_weight,
):
    rows_here, cols_here, chan_here = pair.shape
    residues = cols_here * lax.axis_size(("col", "sub"))
    row_offset = lax.axis_index("row") * rows_here
    col_offset = lax.axis_index(("col", "sub")) * cols_here
    residue_live = residue_mask.astype(jnp.float32)
    live_rows = lax.dynamic_slice_in_dim(residue_live, row_offset, rows_here)
    live_cols = lax.dynamic_slice_in_dim(residue_live, col_offset, cols_here)
    pair_live = (live_rows[:, None] * live_cols[None, :])[:, :, None]
    tri_normed = norm_last(pair, tri_norm_gain).astype(jnp.bfloat16)
    in_width = tri_in_weight.shape[2]
    projected = project(tri_normed, tri_in_weight.reshape(tri_in_weight.shape[0], -1)).reshape(
        rows_here, cols_here, 4, in_width
    )
    left_factor = (jax.nn.sigmoid(projected[:, :, 0]) * projected[:, :, 1] * pair_live).astype(
        jnp.bfloat16
    )
    right_factor = (jax.nn.sigmoid(projected[:, :, 2]) * projected[:, :, 3] * pair_live).astype(
        jnp.bfloat16
    )
    terms = jnp.einsum(
        "ikh,jkh->ijh",
        left_factor,
        lax.all_gather(right_factor, "row", axis=0, tiled=True),
        preferred_element_type=jnp.float32,
    )
    tri_sum = sum_at_owner(terms, ("col", "sub"), 1)
    hidden_normed = norm_last(tri_sum, tri_out_norm_gain).astype(jnp.bfloat16)
    tri_gate = jax.nn.sigmoid(project(tri_normed, tri_gate_weight))
    pair_mid = pair + tri_gate * project(hidden_normed, tri_out_weight)
    att_normed = norm_last(pair_mid, att_norm_gain).astype(jnp.bfloat16)
    head_width = att_proj_weight.shape[2]
    heads_here = att_bias_weight.shape[1]
    head_size = head_width // heads_here
    projected = project(att_normed, att_proj_weight.reshape(att_proj_weight.shape[0], -1)).reshape(
        rows_here, cols_here, 4, head_width
    )
    queries = (projected[:, :, 0] * head_size ** (-0.5)).astype(jnp.bfloat16)
    key_rows = projected[:, :, 1].astype(jnp.bfloat16)
    value_rows = projected[:, :, 2].astype(jnp.bfloat16)
    att_gate = jax.nn.sigmoid(projected[:, :, 3])
    pair_bias = project(att_normed, att_bias_weight).astype(jnp.bfloat16)
    key_all, value_all = in_one_piece((key_rows, value_rows), ("col", "sub"), 1, 0)
    bias_all_rows = gathered_copies(pair_bias, "row", 0)
    bias_panel = lax.all_to_all(
        bias_all_rows, ("col", "sub"), split_axis=0, concat_axis=1, tiled=True
    )
    mask_row = (residue_live - 1.0) * mask_penalty
    head_bias = jnp.transpose(bias_panel.astype(jnp.float32), (2, 0, 1)) + mask_row[None, None, :]
    block_rows = math.gcd(rows_here, max(1, 512 // cols_here))
    blocks = rows_here // block_rows

    def attend(block_items):
        query_block, key_block, value_block = block_items
        scores = (
            jnp.einsum(
                "ijhd,ikhd->ihjk", query_block, key_block, preferred_element_type=jnp.float32
            )
            + head_bias[None]
        )
        row_max = jnp.max(scores, axis=-1, keepdims=True)
        raised = jnp.exp(scores - row_max)
        weights = (raised / jnp.sum(raised, axis=-1, keepdims=True)).astype(jnp.bfloat16)
        return jnp.einsum(
            "ihjk,ikhd->ijhd", weights, value_block, preferred_element_type=jnp.float32
        )

    attended = lax.map(
        attend,
        (
            queries.reshape(blocks, block_rows, cols_here, heads_here, head_size),
            key_all.reshape(blocks, block_rows, residues, heads_here, head_size),
            value_all.reshape(blocks, block_rows, residues, heads_here, head_size),
        ),
    )
    gated = (attended.reshape(rows_here, cols_here, head_width) * att_gate).astype(jnp.bfloat16)
    return pair_mid + project(gated, att_out_weight)


def solution(mesh):
    placed = (
        P(("parts", "row"), ("col", "sub"), None),
        P("parts"),
        P(),
        P(),
        P(),
        P(),
        P(),
        P(),
        P(),
        P(),
        P(),
    )
    return jax.shard_map(
        body,
        mesh=mesh,
        in_specs=placed,
        out_specs=P(("parts", "row"), ("col", "sub"), None),
        check_vma=False,
    )
```

profile of v0, /device:TPU:33, one launch (start us, length us, event | category | flops | bytes accessed | tf_op | source)
XLA Modules:
  0.0 341.0 jit_solution(17317028375399813214)
XLA Ops:
  6.6 0.7 convert_element_type.59
  7.5 1.1 reduce_sum.72
  8.6 1.2 multiply_reduce_fusion.2
  9.8 0.9 copy.126
  11.3 0.8 fusion.33
  12.3 1.2 copy.102
  13.5 147.5 %all-gather.3.cloned.1.call-done = bf16[384,48,128]{2,1,0:T(8,128)(2,1)} async-done(((bf16[12,48,128]{2,1,0:T(8,128)(2,1)}), bf16[384,48,128]{2,1,0:T(8,128)(2,1)}) %all-gather.3.cloned.1.call-update) | async-done | bytes 4718608 | tf_op jit(solution)/shard_map/all_gather | solution.py:94
  160.9 17.8 %copy.101 = bf16[384,48,128]{1,0,2:T(8,128)(2,1)} copy(bf16[384,48,128]{2,1,0:T(8,128)(2,1)} %all-gather.3.cloned.1.call-done) | data formatting | bytes 9437184 | tf_op jit(solution)/shard_map/all_gather | solution.py:94
  178.7 9.1 %convolution_bitcast_fusion.1 = f32[12,384,128]{1,0,2:T(8,128)S(1)} fusion(bf16[384,48,128]{1,0,2:T(8,128)(2,1)} %copy.101, bf16[12,48,128]{1,0,2:T(8,128)(2,1)} %copy.102), kind=kOutput, calls=%fused_computation.18 | convolution fusion | flops 56623104 | bytes 7225344 | tf_op jit(solution)/shard_map/ikh,jkh->ijh/dot_general | solution.py:91
  187.8 2.1 copy.103
  190.0 3.3 copy.104
  193.2 23.9 %all-to-all-start = ((f32[8,12,48,128]{3,2,1,0:T(8,128)}), f32[8,12,48,128]{3,2,1,0:T(8,128)S(1)}, u32[]{:S(2)}, u32[]{:S(2)}) async-start(f32[8,12,48,128]{3,2,1,0:T(8,128)} %copy.104), calls=%async_computation | async-start | bytes 4718592 | tf_op jit(solution)/shard_map/all_to_all | solution.py:19
  217.7 28.5 %all-to-all-done = f32[8,12,48,128]{3,2,1,0:T(8,128)S(1)} async-done(((f32[8,12,48,128]{3,2,1,0:T(8,128)}), f32[8,12,48,128]{3,2,1,0:T(8,128)S(1)}, u32[]{:S(2)}, u32[]{:S(2)}) %all-to-all-start) | async-done | bytes 2359328 | tf_op jit(solution)/shard_map/all_to_all | solution.py:19
  247.9 0.7 pad_maximum_fusion
  249.2 1.2 reshape.185
  250.4 12.5 %all-to-all-start.1 = ((bf16[32,2,1152]{2,1,0:T(2,128)(2,1)}), bf16[32,2,1152]{2,1,0:T(2,128)(2,1)S(1)}, u32[]{:S(2)}, u32[]{:S(2)}) async-start(bf16[32,2,1152]{2,1,0:T(2,128)(2,1)} %reshape.185), calls=%async_computation.1 | async-start | bytes 294912 | tf_op jit(solution)/shard_map/all_to_all | solution.py:32
  263.0 30.6 %all-to-all-done.1 = bf16[32,2,1152]{2,1,0:T(2,128)(2,1)S(1)} async-done(((bf16[32,2,1152]{2,1,0:T(2,128)(2,1)}), bf16[32,2,1152]{2,1,0:T(2,128)(2,1)S(1)}, u32[]{:S(2)}, u32[]{:S(2)}) %all-to-all-start.1) | async-done | bytes 147488 | tf_op jit(solution)/shard_map/all_to_all | solution.py:32
  293.9 1.2 reshape.187
  295.1 5.9 %all-to-all-start.2 = ((bf16[8,2,4608]{2,1,0:T(2,128)(2,1)}), bf16[8,2,4608]{2,1,0:T(2,128)(2,1)S(1)}, u32[]{:S(2)}, u32[]{:S(2)}) async-start(bf16[8,2,4608]{2,1,0:T(2,128)(2,1)} %reshape.187), calls=%async_computation.2 | async-start | bytes 294912 | tf_op jit(solution)/shard_map/all_to_all | solution.py:115
  301.3 5.2 %all-to-all-done.2 = bf16[8,2,4608]{2,1,0:T(2,128)(2,1)S(1)} async-done(((bf16[8,2,4608]{2,1,0:T(2,128)(2,1)}), bf16[8,2,4608]{2,1,0:T(2,128)(2,1)S(1)}, u32[]{:S(2)}, u32[]{:S(2)}) %all-to-all-start.2) | async-done | bytes 147488 | tf_op jit(solution)/shard_map/all_to_all | solution.py:115
  308.1 1.8 fusion.68
  309.9 1.4 copy.107
  311.3 0.7 copy.109
  312.1 18.8 %while.10 = (s32[]{:T(128)}, f32[6,2,48,4,32]{2,4,3,1,0:T(8,128)}, bf16[6,2,384,4,32]{2,4,3,1,0:T(8,128)(2,1)}, bf16[6,2,48,4,32]{2,4,3,1,0:T(8,128)(2,1)S(1)}, ...) while((s32[]{:T(128)}, f32[6,2,48,4,32]{2,4,3,1,0:T(8,128)}, ...), condition=%wide.region_10.11_spmd, body=%wide.region_7.10_spmd.sunk | while | flops 29344896 | bytes 3220045 | solution.py:138
  312.8 2.4 fusion.91
  316.0 2.4 fusion.91
  319.1 2.4 fusion.91
  322.2 2.4 fusion.91
  325.4 2.4 fusion.91
  328.5 2.4 fusion.91
  330.9 1.4 copy.113
  332.3 1.9 convolution_add_fusion.1
  (72 shorter events, 10.1 us)
Async XLA Ops:
  6.5 240.2 %copy-start = (bf16[128,128]{1,0:T(8,128)(2,1)S(1)}, bf16[128,128]{1,0:T(8,128)(2,1)}, u32[]{:S(2)}) copy-start(bf16[128,128]{1,0:T(8,128)(2,1)} %param.19) | copy-start | bytes 98308
  6.6 4.4 %copy-start.1 = (f32[12,48,128]{2,1,0:T(8,128)S(1)}, f32[12,48,128]{2,1,0:T(8,128)}, u32[]{:S(2)}) copy-start(f32[12,48,128]{2,1,0:T(8,128)} %param.13) | copy-start | bytes 884740
  6.6 4.4 %copy-start.7 = (f32[128]{0:T(128)S(1)}, f32[128]{0:T(128)}, u32[]{:S(2)}) copy-start(f32[128]{0:T(128)} %param.15) | copy-start | bytes 1540
  6.6 154.4 %all-gather.3.cloned.1.call-start = ((), (), s32[]{:S(2)}) async-start(), calls=%async_computation.3 | async-start | bytes 4866048 | tf_op jit(solution)/shard_map/all_gather | solution.py:94
  193.2 24.0 %copy-start.3 = (bf16[128,4,128]{2,1,0:T(4,128)(2,1)S(1)}, bf16[128,4,128]{2,1,0:T(4,128)(2,1)}, u32[]{:S(2)}) copy-start(bf16[128,4,128]{2,1,0:T(4,128)(2,1)} %param.21) | copy-start | bytes 393220
  193.2 24.1 %copy-start.9 = (bf16[128,128]{1,0:T(8,128)(2,1)S(1)}, bf16[128,128]{1,0:T(8,128)(2,1)}, u32[]{:S(2)}) copy-start(bf16[128,128]{1,0:T(8,128)(2,1)} %param.17) | copy-start | bytes 98308
  193.2 53.0 %all-to-all-start = ((f32[8,12,48,128]{3,2,1,0:T(8,128)}), f32[8,12,48,128]{3,2,1,0:T(8,128)S(1)}, u32[]{:S(2)}, u32[]{:S(2)}) async-start(f32[8,12,48,128]{3,2,1,0:T(8,128)} %copy.104), calls=%async_computation | async-start | bytes 4718592 | tf_op jit(solution)/shard_map/all_to_all | solution.py:19
  217.2 90.9 %all-gather.5.cloned.1.call-start = ((), (), s32[]{:S(2)}) async-start(), calls=%async_computation.4 | async-start | bytes 2654208 | tf_op jit(solution)/shard_map/all_gather | solution.py:26
  217.7 29.0 %copy-start.8 = (f32[128]{0:T(128)S(1)}, f32[128]{0:T(128)}, u32[]{:S(2)}) copy-start(f32[128]{0:T(128)} %param.18) | copy-start | bytes 1540
  246.4 1.1 copy-start.5
  247.9 53.2 %copy-start.2 = (f32[12,48,4,128]{3,1,2,0:T(8,128)}, f32[12,48,4,128]{3,1,2,0:T(8,128)S(1)}, u32[]{:S(2)}) copy-start(f32[12,48,4,128]{3,1,2,0:T(8,128)S(1)} %get-tuple-element.67) | copy-start | bytes 3538948
  247.9 0.9 copy-start.6
  247.9 15.0 %copy-start.4 = (s32[384]{0:T(512)S(1)}, s32[384]{0:T(512)}, u32[]{:S(2)}) copy-start(s32[384]{0:T(512)} %param.14) | copy-start | bytes 4612
  250.4 43.1 %all-to-all-start.1 = ((bf16[32,2,1152]{2,1,0:T(2,128)(2,1)}), bf16[32,2,1152]{2,1,0:T(2,128)(2,1)S(1)}, u32[]{:S(2)}, u32[]{:S(2)}) async-start(bf16[32,2,1152]{2,1,0:T(2,128)(2,1)} %reshape.185), calls=%async_computation.1 | async-start | bytes 294912 | tf_op jit(solution)/shard_map/all_to_all | solution.py:32
  295.1 11.4 %all-to-all-start.2 = ((bf16[8,2,4608]{2,1,0:T(2,128)(2,1)}), bf16[8,2,4608]{2,1,0:T(2,128)(2,1)S(1)}, u32[]{:S(2)}, u32[]{:S(2)}) async-start(bf16[8,2,4608]{2,1,0:T(2,128)(2,1)} %reshape.187), calls=%async_computation.2 | async-start | bytes 294912 | tf_op jit(solution)/shard_map/all_to_all | solution.py:115
  312.0 20.2 %copy-start.10 = (bf16[128,128]{1,0:T(8,128)(2,1)S(1)}, bf16[128,128]{1,0:T(8,128)(2,1)}, u32[]{:S(2)}) copy-start(bf16[128,128]{1,0:T(8,128)(2,1)} %param.23) | copy-start | bytes 98308
Sparse Core Ops, SparseCore 0:
  12.4 148.5 all-gather.2
  248.9 31.5 all-gather.4
where the time goes:
time: 342 us; the launch traced here: 341 us
  waiting for transfers between devices  212 us (62%)
  starting transfers between devices  42.3 us (12%)
  local copies, waits for them, and re-layouts  35.8 us (10%)
  matrix products  31.6 us (9%)
  between operations  13.8 us (4%)
  other arithmetic  5.57 us (2%)
    all_gather x1, waiting for transfers between devices, body(): lax.all_gather(right_factor, 'row', axis=0, tiled=True)  147 us
    all_to_all x1, waiting for transfers between devices, from_everyone(): return lax.all_to_all(copies, axis, split_axis=0, concat_axis=0, tiled=True)  30.6 us
    all_to_all x1, waiting for transfers between devices, sum_at_owner(): lax.all_to_all(split_up(array, dim, devices), axis, 0, 0, tiled=True)  28.5 us
    all_to_all x1, starting transfers between devices, sum_at_owner(): lax.all_to_all(split_up(array, dim, devices), axis, 0, 0, tiled=True)  23.9 us
    all_gather x1, local copies, waits for them, and re-layouts, body(): lax.all_gather(right_factor, 'row', axis=0, tiled=True)  17.8 us
    dot_general x6, matrix products, attend(): jnp.einsum('ihjk,ikhd->ijhd', weights, value_block, preferred_element_typ...  14.3 us
    all_to_all x1, starting transfers between devices, from_everyone(): return lax.all_to_all(copies, axis, split_axis=0, concat_axis=0, tiled=True)  12.5 us
    dot_general x1, matrix products, body(): jnp.einsum('ikh,jkh->ijh', left_factor, lax.all_gather(right_factor, 'row...  9.08 us
  transfers between devices with their start and end apart: 5, of which 4 were waited for; matrix products, arithmetic and copies ran while one was open for 2% of the time, Pallas kernels for 0%

commit v1 on v0

--- a/solution.py
+++ b/solution.py
@@ -6,6 +6,13 @@
 
 epsilon = 1e-05
 mask_penalty = 1000000000.0
+
+
+def swapped_in(x, axis, dim):
+    size = lax.axis_size(axis)
+    blocks = jnp.stack([x for _ in range(size)])
+    blocks = lax.all_to_all(blocks, axis, split_axis=0, concat_axis=0)
+    return jnp.concatenate(blocks, axis=dim)
 
 
 def split_up(array, dim, devices):
@@ -91,7 +98,7 @@
     terms = jnp.einsum(
         "ikh,jkh->ijh",
         left_factor,
-        lax.all_gather(right_factor, "row", axis=0, tiled=True),
+        swapped_in(right_factor, "row", 0),
         preferred_element_type=jnp.float32,
     )
     tri_sum = sum_at_owner(terms, ("col", "sub"), 1)

time: 342 us -> 637 us (1.86)
  waiting for transfers between devices: 212 us -> 469 us
  starting transfers between devices: 42.3 us -> 78.9 us
    all_to_all x0 -> x1, waiting for transfers between devices: none -> 405 us  [swapped_in(): blocks = lax.all_to_all(blocks, axis, split_axis=0, concat_axis=0)]
    all_gather x1 -> x0, waiting for transfers between devices: 147 us -> none  [body(): lax.all_gather(right_factor, 'row', axis=0, tiled=True)]
    all_to_all x0 -> x1, starting transfers between devices: none -> 46.3 us  [swapped_in(): blocks = lax.all_to_all(blocks, axis, split_axis=0, concat_axis=0)]
    all_to_all x1, starting transfers between devices: 23.9 us -> 5.57 us  [sum_at_owner(): lax.all_to_all(split_up(array, dim, devices), axis, 0, 0, tiled=True)]
    all_gather x1 -> x0, local copies, waits for them, and re-layouts: 17.8 us -> none  [body(): lax.all_gather(right_factor, 'row', axis=0, tiled=True)]
    all_to_all x1, starting transfers between devices: 12.5 us -> 21.1 us  [from_everyone(): return lax.all_to_all(copies, axis, split_axis=0, concat_axis=0, tiled=True)]
    reshape x0 -> x1, local copies, waits for them, and re-layouts: none -> 7.59 us  [swapped_in(): return jnp.concatenate(blocks, axis=dim)]
  transfers between devices with their start and end apart: 5 -> 5, of which waited for: 4 -> 4; matrix products, arithmetic and copies ran while one was open for 2% -> 1% of each run, Pallas kernels for 0% -> 0%
where the time goes in v1:
time: 637 us; the launch traced here: 635 us
  waiting for transfers between devices  469 us (74%)
  starting transfers between devices  78.9 us (12%)
  matrix products  37 us (6%)
  local copies, waits for them, and re-layouts  31.5 us (5%)
  between operations  13.8 us (2%)
    all_to_all x1, waiting for transfers between devices, swapped_in(): blocks = lax.all_to_all(blocks, axis, split_axis=0, concat_axis=0)  405 us
    all_to_all x1, starting transfers between devices, swapped_in(): blocks = lax.all_to_all(blocks, axis, split_axis=0, concat_axis=0)  46.3 us
    all_to_all x1, waiting for transfers between devices, from_everyone(): return lax.all_to_all(copies, axis, split_axis=0, concat_axis=0, tiled=True)  30.6 us
    all_to_all x1, waiting for transfers between devices, sum_at_owner(): lax.all_to_all(split_up(array, dim, devices), axis, 0, 0, tiled=True)  28.5 us
    all_to_all x1, starting transfers between devices, from_everyone(): return lax.all_to_all(copies, axis, split_axis=0, concat_axis=0, tiled=True)  21.1 us
    dot_general x6, matrix products, attend(): jnp.einsum('ihjk,ikhd->ijhd', weights, value_block, preferred_element_typ...  14.3 us
  transfers between devices with their start and end apart: 5, of which 4 were waited for; matrix products, arithmetic and copies ran while one was open for 1% of the time, Pallas kernels for 0%

profile of v1, /device:TPU:33, one launch (start us, length us, event | category | flops | bytes accessed | tf_op | source)
XLA Modules:
  0.0 635.4 jit_solution(18206508943255735724)
XLA Ops:
  8.6 1.2 multiply_reduce_fusion.2
  11.5 3.2 stack.2
  14.8 46.3 %all-to-all-start = ((bf16[32,12,48,128]{3,2,1,0:T(8,128)(2,1)}), bf16[32,12,48,128]{3,2,1,0:T(8,128)(2,1)}, u32[]{:S(2)}, u32[]{:S(2)}) async-start(bf16[32,12,48,128]{3,2,1,0:T(8,128)(2,1)} %stack.2), calls=%async_computation | async-start | bytes 9437184 | tf_op jit(solution)/shard_map/all_to_all | solution.py:14
  62.3 405.0 %all-to-all-done = bf16[32,12,48,128]{3,2,1,0:T(8,128)(2,1)} async-done(((bf16[32,12,48,128]{3,2,1,0:T(8,128)(2,1)}), bf16[32,12,48,128]{3,2,1,0:T(8,128)(2,1)}, u32[]{:S(2)}, u32[]{:S(2)}) %all-to-all-start) | async-done | bytes 4718624 | tf_op jit(solution)/shard_map/all_to_all | solution.py:14
  467.2 7.6 %copy.101 = bf16[384,48,128]{0,1,2:T(8,128)(2,1)} copy(bf16[384,48,128]{2,1,0:T(8,128)(2,1)} %bitcast.12) | data formatting | bytes 9437184 | tf_op jit(solution)/shard_map/reshape | solution.py:15
  474.8 3.4 convolution_bitcast_fusion.1
  478.2 2.1 copy.103
  480.4 3.3 copy.104
  483.6 5.6 all-to-all-start.1
  489.7 28.5 %all-to-all-done.1 = f32[8,12,48,128]{3,2,1,0:T(8,128)S(1)} async-done(((f32[8,12,48,128]{3,2,1,0:T(8,128)}), f32[8,12,48,128]{3,2,1,0:T(8,128)S(1)}, u32[]{:S(2)}, u32[]{:S(2)}) %all-to-all-start.1) | async-done | bytes 2359328 | tf_op jit(solution)/shard_map/all_to_all | solution.py:26
  522.5 21.1 %all-to-all-start.2 = ((bf16[32,2,1152]{2,1,0:T(2,128)(2,1)}), bf16[32,2,1152]{2,1,0:T(2,128)(2,1)S(1)}, u32[]{:S(2)}, u32[]{:S(2)}) async-start(bf16[32,2,1152]{2,1,0:T(2,128)(2,1)} %reshape.194), calls=%async_computation.2 | async-start | bytes 294912 | tf_op jit(solution)/shard_map/all_to_all | solution.py:39
  543.6 30.6 %all-to-all-done.2 = bf16[32,2,1152]{2,1,0:T(2,128)(2,1)S(1)} async-done(((bf16[32,2,1152]{2,1,0:T(2,128)(2,1)}), bf16[32,2,1152]{2,1,0:T(2,128)(2,1)S(1)}, u32[]{:S(2)}, u32[]{:S(2)}) %all-to-all-start.2) | async-done | bytes 147488 | tf_op jit(solution)/shard_map/all_to_all | solution.py:39
  575.8 5.9 all-to-all-start.3
  581.9 5.2 all-to-all-done.3
  588.7 2.8 fusion.68
  591.6 2.4 copy.107
  593.9 1.4 copy.109
  595.3 30.0 %while.10 = (s32[]{:T(128)}, f32[6,2,48,4,32]{2,4,3,1,0:T(8,128)}, bf16[6,2,384,4,32]{2,4,3,1,0:T(8,128)(2,1)}, bf16[6,2,48,4,32]{2,4,3,1,0:T(8,128)(2,1)S(1)}, ...) while((s32[]{:T(128)}, f32[6,2,48,4,32]{2,4,3,1,0:T(8,128)}, ...), condition=%wide.region_10.11_spmd, body=%wide.region_7.10_spmd.sunk | while | flops 29344896 | bytes 3220045 | solution.py:145
  596.6 1.4 fusion.90
  597.9 2.4 fusion.91
  601.6 1.4 fusion.90
  602.9 2.4 fusion.91
  606.5 1.4 fusion.90
  607.9 2.4 fusion.91
  611.5 1.4 fusion.90
  612.9 2.4 fusion.91
  616.5 1.4 fusion.90
  617.9 2.4 fusion.91
  621.5 1.4 fusion.90
  622.9 2.4 fusion.91
  625.3 1.4 copy.113
  626.7 1.9 convolution_add_fusion.1
  (72 shorter events, 20.2 us)
Async XLA Ops:
  6.5 512.2 %copy-start = (bf16[128,128]{1,0:T(8,128)(2,1)S(1)}, bf16[128,128]{1,0:T(8,128)(2,1)}, u32[]{:S(2)}) copy-start(bf16[128,128]{1,0:T(8,128)(2,1)} %param.19) | copy-start | bytes 98308
  6.6 4.4 copy-start.1
  6.6 4.4 copy-start.7
  14.8 452.5 %all-to-all-start = ((bf16[32,12,48,128]{3,2,1,0:T(8,128)(2,1)}), bf16[32,12,48,128]{3,2,1,0:T(8,128)(2,1)}, u32[]{:S(2)}, u32[]{:S(2)}) async-start(bf16[32,12,48,128]{3,2,1,0:T(8,128)(2,1)} %stack.2), calls=%async_computation | async-start | bytes 9437184 | tf_op jit(solution)/shard_map/all_to_all | solution.py:14
  483.6 5.6 copy-start.3
  483.6 5.7 copy-start.9
  483.6 34.6 %all-to-all-start.1 = ((f32[8,12,48,128]{3,2,1,0:T(8,128)}), f32[8,12,48,128]{3,2,1,0:T(8,128)S(1)}, u32[]{:S(2)}, u32[]{:S(2)}) async-start(f32[8,12,48,128]{3,2,1,0:T(8,128)} %copy.104), calls=%async_computation.1 | async-start | bytes 4718592 | tf_op jit(solution)/shard_map/all_to_all | solution.py:26
  489.2 99.5 %all-gather.2.cloned.1.call-start = ((), (), s32[]{:S(2)}) async-start(), calls=%async_computation.4 | async-start | bytes 2654208 | tf_op jit(solution)/shard_map/all_gather | solution.py:33
  489.7 29.0 %copy-start.8 = (f32[128]{0:T(128)S(1)}, f32[128]{0:T(128)}, u32[]{:S(2)}) copy-start(f32[128]{0:T(128)} %param.18) | copy-start | bytes 1540
  518.4 1.1 copy-start.5
  519.9 61.8 %copy-start.2 = (f32[12,48,4,128]{3,1,2,0:T(8,128)}, f32[12,48,4,128]{3,1,2,0:T(8,128)S(1)}, u32[]{:S(2)}) copy-start(f32[12,48,4,128]{3,1,2,0:T(8,128)S(1)} %get-tuple-element.67) | copy-start | bytes 3538948
  519.9 0.9 copy-start.6
  519.9 23.6 %copy-start.4 = (s32[384]{0:T(512)S(1)}, s32[384]{0:T(512)}, u32[]{:S(2)}) copy-start(s32[384]{0:T(512)} %param.14) | copy-start | bytes 4612
  522.5 51.7 %all-to-all-start.2 = ((bf16[32,2,1152]{2,1,0:T(2,128)(2,1)}), bf16[32,2,1152]{2,1,0:T(2,128)(2,1)S(1)}, u32[]{:S(2)}, u32[]{:S(2)}) async-start(bf16[32,2,1152]{2,1,0:T(2,128)(2,1)} %reshape.194), calls=%async_computation.2 | async-start | bytes 294912 | tf_op jit(solution)/shard_map/all_to_all | solution.py:39
  575.8 11.4 %all-to-all-start.3 = ((bf16[8,2,4608]{2,1,0:T(2,128)(2,1)}), bf16[8,2,4608]{2,1,0:T(2,128)(2,1)S(1)}, u32[]{:S(2)}, u32[]{:S(2)}) async-start(bf16[8,2,4608]{2,1,0:T(2,128)(2,1)} %reshape.196), calls=%async_computation.3 | async-start | bytes 294912 | tf_op jit(solution)/shard_map/all_to_all | solution.py:122
  595.3 31.3 %copy-start.10 = (bf16[128,128]{1,0:T(8,128)(2,1)S(1)}, bf16[128,128]{1,0:T(8,128)(2,1)}, u32[]{:S(2)}) copy-start(bf16[128,128]{1,0:T(8,128)(2,1)} %param.23) | copy-start | bytes 98308
Sparse Core Ops, SparseCore 0:
  520.9 40.6 all-gather.1
